TPU v7x, 256 devices: a whole 4x4x8 slice. The times are simulated.
256 devices in a mesh: segment: 4 (over x), lane: 64 (over y, z, core).
Axes of the slice: x: 4, y: 4, z: 8, core: 2. Of those that a mesh axis runs over, the one named last changes fastest.
Arguments:
- spectra: float32 [4, 4096, 1024], P(None, 'lane'), may hold values from -6 to 6
- rfi_flags: int32 [4, 4096, 8], P(None, 'lane'), may hold values 0 or 1
- sub_delay: int32 [64, 4096], P(None, 'lane'), may hold values from 0 to 7
- fine_delay: int32 [2048, 64], P('lane'), may hold values from 0 to 31
- widths: int32 [8], replicated, may hold values from 1 to 64
Outputs:
- peaks: float32 [4, 2048, 8], P('segment', 'lane')
All inputs are finite; a program needn't handle non-finite values. No bound on the sum of `rfi_flags` on one device may be relied on, other than what follows from the above.
Results may differ from a plain program's by a relative error of at most 0.0001.
Values sent between devices are 32-bit elements; how exact they have to be, the bound alone decides.
No kernel may reach another device: no remote copies, remote signals or barrier semaphores. Data moves between devices by JAX's collectives and lax.ppermute only.
A program may use at most 64 MiB of HBM per device.

v0:
```python
import jax
import jax.numpy as jnp
from jax import lax
from jax.sharding import PartitionSpec as P

C = 4096
SUBCH = 64
NSUB = 64
NCOARSE = 64
NDM = 2048
D1 = 8
D2 = 32


delay_group = 4


def sent_to_all(shard, axis):
    copies = jnp.broadcast_to(shard, (lax.axis_size(axis), *shard.shape))
    return lax.all_to_all(copies, axis, split_axis=0, concat_axis=0, tiled=True)


def of_everyone(shard, axis):
    return sent_to_all(shard, axis).sum(axis=0)


def clean_block(power_in, flag_rows, block_len):
    row_count, samples = power_in.shape
    kept_mask = 1.0 - flag_rows.astype(jnp.float32)
    kept_mask = jnp.broadcast_to(
        kept_mask[:, :, None], (row_count, flag_rows.shape[1], block_len)
    ).reshape(row_count, samples)
    masked = kept_mask * power_in
    centre = jnp.mean(masked, axis=1, keepdims=True)
    spread = jnp.mean((masked - centre) * (masked - centre), axis=1, keepdims=True)
    return kept_mask * (power_in - centre) * lax.rsqrt(spread + 1e-05)


def detect(centered, widths, total_sq, cell_count):
    sigma = jnp.sqrt(total_sq / cell_count + 1e-06)
    samples = centered.shape[1]
    prefix = jnp.concatenate(
        [jnp.zeros((centered.shape[0], 1), jnp.float32), jnp.cumsum(centered, axis=1)], axis=1
    )
    sample_idx = jnp.arange(samples, dtype=jnp.int32)
    ends = jnp.minimum(sample_idx[None, :] + widths[:, None], samples)
    upper = prefix[:, ends]
    lower = prefix[:, None, :samples]
    scaled = (upper - lower) / (sigma * jnp.sqrt(widths.astype(jnp.float32)))[None, :, None]
    return jnp.max(scaled, axis=2)


def subband_sums(cleaned, sub_delay, sub_width, delays):
    row_count, samples = cleaned.shape
    groups = row_count // sub_width
    coarse = sub_delay.shape[0]
    levels = jnp.arange(delays, dtype=jnp.int32)
    onehot = (
        sub_delay.reshape(coarse, groups, 1, sub_width) == levels[None, None, :, None]
    ).astype(jnp.float32)
    weights_all = onehot.transpose(1, 0, 2, 3)
    padded = jnp.pad(cleaned.reshape(groups, sub_width, samples), ((0, 0), (0, 0), (0, delays)))
    totals = jnp.zeros((coarse, groups, samples), jnp.float32)
    for first_lag in range(0, delays, delay_group):
        span_here = min(delay_group, delays - first_lag)
        stacked = jnp.stack(
            [
                padded[:, :, first_lag + offset : first_lag + offset + samples]
                for offset in range(span_here)
            ],
            axis=1,
        )
        stacked = stacked.reshape(groups, span_here * sub_width, samples)
        weights = weights_all[:, :, first_lag : first_lag + span_here, :].reshape(
            groups, coarse, span_here * sub_width
        )
        totals = totals + jnp.einsum(
            "bkx,bxs->kbs", weights, stacked, precision=lax.Precision.HIGHEST
        )
    return (totals, jnp.sum(onehot, axis=3))


def fine_sums(source, onehot):
    groups, bands, samples = source.shape
    per_group = onehot.shape[1]
    delays = onehot.shape[2]
    padded = jnp.pad(source, ((0, 0), (0, 0), (0, delays)))
    running = jnp.zeros((groups, per_group, samples), jnp.float32)
    for first_lag in range(0, delays, delay_group):
        span_here = min(delay_group, delays - first_lag)
        stacked = jnp.stack(
            [
                padded[:, :, first_lag + offset : first_lag + offset + samples]
                for offset in range(span_here)
            ],
            axis=1,
        )
        stacked = stacked.reshape(groups, span_here * bands, samples)
        weights = onehot[:, :, first_lag : first_lag + span_here, :].reshape(
            groups, per_group, span_here * bands
        )
        running = running + jnp.einsum(
            "gjx,gxs->gjs", weights, stacked, precision=lax.Precision.HIGHEST
        )
    return running.reshape(groups * per_group, samples)


def body(spectra, rfi_flags, sub_delay, fine_delay, widths):
    lane_count = lax.axis_size("lane")
    section_count = lax.axis_size("segment")
    section_idx = lax.axis_index("segment")
    batches, row_count, samples = spectra.shape
    block_len = samples // rfi_flags.shape[2]
    coarse_dev = NCOARSE // lane_count
    dm_dev = fine_delay.shape[0]
    per_coarse = dm_dev // coarse_dev
    fine_levels = jnp.arange(D2, dtype=jnp.int32)
    fine_hot = (fine_delay[:, None, :] == fine_levels[None, :, None]).astype(jnp.float32)
    fine_hot = fine_hot.reshape(coarse_dev, per_coarse, D2, NSUB)
    per_section = batches // section_count
    batch_pos = section_idx * per_section + 0
    power_now = lax.dynamic_index_in_dim(spectra, batch_pos, 0, keepdims=False)
    flags_now = lax.dynamic_index_in_dim(rfi_flags, batch_pos, 0, keepdims=False)
    normed = clean_block(power_now, flags_now, block_len)
    channel_sum = of_everyone(jnp.sum(normed, axis=0), "lane")
    cleaned = normed - (channel_sum / C)[None, :]
    totals, counts = subband_sums(cleaned, sub_delay, SUBCH, D1)
    moved = lax.all_to_all(totals, "lane", split_axis=0, concat_axis=1, tiled=True)
    series = fine_sums(moved, fine_hot)
    centered = series - jnp.mean(series, axis=1, keepdims=True)
    total_sq = of_everyone(jnp.sum(centered * centered), "lane")
    outputs = [detect(centered, widths, total_sq, NDM * samples)]
    return jnp.stack(outputs)


def solution(mesh):
    in_specs = (P(None, "lane", None), P(None, "lane", None), P(None, "lane"), P("lane", None), P())
    out_specs = P("segment", "lane", None)
    return jax.shard_map(body, mesh=mesh, in_specs=in_specs, out_specs=out_specs, check_vma=False)
```

profile of v0, /device:TPU:1, one launch (start us, length us, event | category | flops | bytes accessed | tf_op | source)
XLA Modules:
  0.0 108.4 jit_solution(18154578275309590063)
XLA Ops:
  0.0 0.0 copy-start
  0.0 0.8 subtract_bitcast_fusion
  0.8 0.1 copy.22
  0.9 0.1 broadcast_in_dim.8
  1.1 1.1 fusion.111
  2.1 1.2 %multiply_reduce_fusion = f32[64]{0:T(128)S(1)} fusion(f32[64]{0:T(128)S(1)} %broadcast_multiply_fusion.2, f32[1,64,1024]{2,1,0:T(8,128)S(1)} %broadcast_in_dim.9, f32[4,64,1024]{2,1,0:T(8,128)} %param.5, s32[]{:T(128)S(6)} %select_n.16), kind=kLoop, calls=%fused_computation.175 | loop fusion | flops 262080 | bytes 524804 | tf_op jit(solution)/shard_map/reduce_sum | solution.py:35
  3.3 1.1 fusion.123
  4.4 0.8 broadcast_in_dim.10
  5.2 13.1 %all-to-all-start = ((f32[64,1,1024]{2,1,0:T(1,128)}), f32[64,1,1024]{2,1,0:T(1,128)S(1)}, u32[]{:S(2)}, u32[]{:S(2)}) async-start(f32[64,1,1024]{2,1,0:T(1,128)} %broadcast_in_dim.10), calls=%async_computation | async-start | bytes 524288 | tf_op jit(solution)/shard_map/all_to_all | solution.py:20
  18.4 0.8 iota_compare_fusion.1
  19.2 11.1 %all-to-all-done = f32[64,1,1024]{2,1,0:T(1,128)S(1)} async-done(((f32[64,1,1024]{2,1,0:T(1,128)}), f32[64,1,1024]{2,1,0:T(1,128)S(1)}, u32[]{:S(2)}, u32[]{:S(2)}) %all-to-all-start) | async-done | bytes 262176 | tf_op jit(solution)/shard_map/all_to_all | solution.py:20
  30.3 0.2 reduce_sum.66
  30.5 0.0 copy-done
  30.5 0.1 broadcast_subtract_fusion
  30.7 0.0 copy-start.2
  30.7 0.0 copy-start.1
  30.7 0.5 fusion.101
  31.2 0.1 fusion.110
  31.3 0.5 convolution_bitcast_fusion
  31.9 0.5 fusion.2
  32.4 1.0 copy.24
  33.4 6.0 %all-to-all-start.1 = ((f32[64,1,1024]{2,1,0:T(1,128)}), f32[64,1,1024]{2,1,0:T(1,128)S(1)}, u32[]{:S(2)}, u32[]{:S(2)}) async-start(f32[64,1,1024]{2,1,0:T(1,128)} %copy.24), calls=%async_computation.1 | async-start | bytes 524288 | tf_op jit(solution)/shard_map/all_to_all | solution.py:128
  39.4 0.0 copy-done.2
  39.5 0.1 fusion.112
  39.5 0.0 copy-done.1
  39.6 0.1 iota_compare_fusion
  39.6 11.8 %all-to-all-done.1 = f32[64,1,1024]{2,1,0:T(1,128)S(1)} async-done(((f32[64,1,1024]{2,1,0:T(1,128)}), f32[64,1,1024]{2,1,0:T(1,128)S(1)}, u32[]{:S(2)}, u32[]{:S(2)}) %all-to-all-start.1) | async-done | bytes 262176 | tf_op jit(solution)/shard_map/all_to_all | solution.py:128
  51.5 1.4 %fusion.70 = (f32[1,1,64,1024]{3,2,1,0:T(8,128)S(1)}, f32[1,1,64,1024]{3,2,1,0:T(8,128)S(1)}, f32[1,1,64,1024]{3,2,1,0:T(8,128)S(1)}, f32[1,1,64,1024]{3,2,1,0:T...) fusion(f32[1,64,1024]{2,1,0:T(8,128)S(1)} %bitcast.214), kind=kLoop, calls=%fused_computation.131 | loop fusion | bytes 5242880 | tf_op jit(solution)/shard_map/stack | solution.py:91
  52.8 0.9 fusion.89
  53.7 0.5 convolution_bitcast_fusion.8
  54.2 0.5 convolution_bitcast_fusion.7
  54.7 0.5 convolution_bitcast_fusion.6
  55.2 0.5 convolution_bitcast_fusion.5
  55.7 0.5 convolution_bitcast_fusion.4
  56.2 0.5 convolution_bitcast_fusion.3
  56.8 0.5 convolution_bitcast_fusion.2
  57.3 0.6 fusion.124
  57.9 0.7 multiply_reduce_fusion.1
  58.6 0.1 bitcast_subtract_fusion.1
  58.7 9.0 %reduce-window.6 = f32[32,8,128]{2,1,0:T(8,128)S(1)} reduce-window(f32[32,8,128]{2,1,0:T(8,128)S(1)} %bitcast_subtract_fusion.1, f32[]{:T(128)} %constant.21.clone.1), window={size=1x1x128 pad=0_0x0_0x127_0}, to_apply=%region_5.6 | reduce-window | flops 4161536 | bytes 262148 | tf_op jit(solution)/shard_map/reduce-window
  67.8 0.1 slice.218
  67.9 0.1 copy.25
  68.0 0.1 copy.26
  68.1 0.1 broadcast_add_fusion
  68.2 0.2 copy.29
  68.4 1.3 %broadcast_in_dim.11 = f32[64,1,1]{2,1,0:T(1,128)} broadcast(f32[]{:T(128)} %multiply_reduce_fusion.1), dimensions={} | broadcast | bytes 260 | tf_op jit(solution)/shard_map/broadcast_in_dim | solution.py:19
  69.7 6.0 %all-to-all-start.2 = ((f32[64,1,1]{2,1,0:T(1,128)}), f32[64,1,1]{2,1,0:T(1,128)S(1)}, u32[]{:S(2)}, u32[]{:S(2)}) async-start(f32[64,1,1]{2,1,0:T(1,128)} %broadcast_in_dim.11), calls=%async_computation.2 | async-start | bytes 65536 | tf_op jit(solution)/shard_map/all_to_all | solution.py:20
  75.7 0.1 pad_slice_fusion.38
  75.8 0.1 concatenate.3
  75.9 27.7 %gather_fusion = f32[8192,32]{1,0:T(8,128)} fusion(f32[32,1025]{0,1:T(8,128)S(1)} %concatenate.3, s32[8192]{0:T(1024)S(1)} %bitcast_clamp_fusion), kind=kCustom, calls=%fused_computation | custom fusion | bytes 2129920 | tf_op jit(solution)/shard_map/gather | solution.py:47
  103.6 0.0 all-to-all-done.2
  103.6 0.7 reduce_sum.69
  104.9 3.4 %fusion = f32[32,8]{0,1:T(8,128)} fusion(f32[8]{0:T(128)S(1)} %sqrt_multiply_fusion, f32[32,1024]{0,1:T(8,128)S(1)} %pad_slice_fusion.38, f32[8192,32]{1,0:T(8,128)} %gather_fusion), kind=kLoop, calls=%fused_computation.2 | loop fusion | flops 786176 | bytes 1180704 | tf_op jit(solution)/shard_map/reduce_max | solution.py:50
  (12 shorter events, 0.2 us)
Async XLA Ops:
  0.0 30.5 %copy-start = (f32[4,64,1024]{2,1,0:T(8,128)S(1)}, f32[4,64,1024]{2,1,0:T(8,128)}, u32[]{:S(2)}) copy-start(f32[4,64,1024]{2,1,0:T(8,128)} %param.5) | copy-start | bytes 3145732
  5.2 25.1 %all-to-all-start = ((f32[64,1,1024]{2,1,0:T(1,128)}), f32[64,1,1024]{2,1,0:T(1,128)S(1)}, u32[]{:S(2)}, u32[]{:S(2)}) async-start(f32[64,1,1024]{2,1,0:T(1,128)} %broadcast_in_dim.10), calls=%async_computation | async-start | bytes 524288 | tf_op jit(solution)/shard_map/all_to_all | solution.py:20
  30.7 8.8 %copy-start.2 = (s32[8]{0:T(128)S(1)}, s32[8]{0:T(128)}, u32[]{:S(2)}) copy-start(s32[8]{0:T(128)} %param.9) | copy-start | bytes 100
  30.7 8.9 %copy-start.1 = (s32[32,64]{1,0:T(8,128)S(1)}, s32[32,64]{1,0:T(8,128)}, u32[]{:S(2)}) copy-start(s32[32,64]{1,0:T(8,128)} %param.8) | copy-start | bytes 24580
  33.4 18.0 %all-to-all-start.1 = ((f32[64,1,1024]{2,1,0:T(1,128)}), f32[64,1,1024]{2,1,0:T(1,128)S(1)}, u32[]{:S(2)}, u32[]{:S(2)}) async-start(f32[64,1,1024]{2,1,0:T(1,128)} %copy.24), calls=%async_computation.1 | async-start | bytes 524288 | tf_op jit(solution)/shard_map/all_to_all | solution.py:128
  69.7 33.9 %all-to-all-start.2 = ((f32[64,1,1]{2,1,0:T(1,128)}), f32[64,1,1]{2,1,0:T(1,128)S(1)}, u32[]{:S(2)}, u32[]{:S(2)}) async-start(f32[64,1,1]{2,1,0:T(1,128)} %broadcast_in_dim.11), calls=%async_computation.2 | async-start | bytes 65536 | tf_op jit(solution)/shard_map/all_to_all | solution.py:20
where the time goes:
time: 109 us; the launch traced here: 108 us
  local copies, waits for them, and re-layouts  34.5 us (32%)
  starting transfers between devices  25.2 us (23%)
  waiting for transfers between devices  22.9 us (21%)
  other arithmetic  19.5 us (18%)
  matrix products  5.24 us (5%)
    gather x1, local copies, waits for them, and re-layouts, detect(): upper = prefix[:, ends]  27.7 us
    all_to_all x2, starting transfers between devices, sent_to_all(): return lax.all_to_all(copies, axis, split_axis=0, concat_axis=0, tiled=True)  19.2 us
    all_to_all x1, waiting for transfers between devices, body(): lax.all_to_all(totals, 'lane', split_axis=0, concat_axis=1, tiled=True)  11.8 us
    all_to_all x2, waiting for transfers between devices, sent_to_all(): return lax.all_to_all(copies, axis, split_axis=0, concat_axis=0, tiled=True)  11.1 us
    another operation x3, other arithmetic  9.15 us
    all_to_all x1, starting transfers between devices, body(): lax.all_to_all(totals, 'lane', split_axis=0, concat_axis=1, tiled=True)  6.04 us
    dot_general x8, matrix products, fine_sums(): jnp.einsum('gjx,gxs->gjs', weights, stacked, precision=lax.Precision.HIGH...  4.15 us
    reduce_max x1, other arithmetic, detect(): return jnp.max(scaled, axis=2)  3.4 us
  transfers between devices with their start and end apart: 3, of which 2 were waited for; matrix products, arithmetic and copies ran while one was open for 27% of the time, Pallas kernels for 0%

commit v1 on v0

v1 whole, which is shorter than its diff:
```python
import jax
import jax.numpy as jnp
from jax import lax
from jax.experimental import pallas as pl
from jax.experimental.pallas import tpu as pltpu
from jax.sharding import PartitionSpec as P

C = 4096
SUBCH = 64
NSUB = 64
NCOARSE = 64
NDM = 2048
S = 1024
D1 = 8
D2 = 32
NW = 8
JDEV = 32
LANES = 128
NCH = S // LANES
ROW = 2 * NCH + 1
SPLITS = 3
F0 = 2
F1 = D2 // F0


def lane_ids(rows):
    return lax.broadcasted_iota(jnp.int32, (rows, LANES), 1)


def shifted(chunks, amount, lane):
    if amount == 0:
        return chunks
    rolled = [pltpu.roll(c, LANES - amount, axis=1) for c in chunks]
    rolled.append(jnp.zeros_like(rolled[0]))
    return [
        jnp.where(lane < LANES - amount, rolled[c], rolled[c + 1]) for c in range(len(chunks))
    ]


def pieces(x, count):
    parts = []
    for _ in range(count):
        part = x.astype(jnp.bfloat16)
        parts.append(part)
        x = x - part.astype(jnp.float32)
    return parts


def front_kernel(seg_ref, power_ref, flags_ref, delay_ref, out_ref):
    del seg_ref
    keep = 1.0 - flags_ref[0].astype(jnp.float32)
    kept = [jnp.broadcast_to(keep[:, c : c + 1], (SUBCH, LANES)) for c in range(NCH)]
    power = [power_ref[0, :, c * LANES : (c + 1) * LANES] for c in range(NCH)]
    masked = [kept[c] * power[c] for c in range(NCH)]
    centre = jnp.sum(sum(masked), axis=1, keepdims=True) * (1.0 / S)
    spread = sum((m - centre) * (m - centre) for m in masked)
    spread = jnp.sum(spread, axis=1, keepdims=True) * (1.0 / S)
    scale = lax.rsqrt(spread + 1e-05)
    normed = [kept[c] * (power[c] - centre) * scale for c in range(NCH)]

    for c in range(NCH):
        channel_sum = jnp.sum(normed[c], axis=0, keepdims=True)
        out_ref[pl.ds(NCH + c, NCOARSE, stride=ROW), :] = jnp.broadcast_to(
            channel_sum, (NCOARSE, LANES)
        )

    delay = delay_ref[...]
    lane = lane_ids(NCOARSE)
    counts = jnp.zeros((NCOARSE, LANES), jnp.float32)
    for d in range(D1):
        count = jnp.sum((delay == d).astype(jnp.float32), axis=1, keepdims=True)
        counts = jnp.where(
            jnp.logical_and(lane % D1 == d, lane < SPLITS * D1), count, counts
        )
    out_ref[pl.ds(2 * NCH, NCOARSE, stride=ROW), :] = counts

    delay4 = jnp.concatenate([delay] * 4, axis=1)
    weights = jnp.concatenate(
        [(delay4 == d).astype(jnp.float32).astype(jnp.bfloat16) for d in range(D1)], axis=0
    )
    split = [pieces(n, SPLITS) for n in normed]
    rows = [
        jnp.concatenate([split[c][s] for c in range(NCH)], axis=1) for s in range(SPLITS)
    ]
    rows.append(jnp.zeros_like(rows[0]))
    data = jnp.concatenate(rows, axis=0)
    sums = jnp.dot(weights, data, preferred_element_type=jnp.float32)
    totals = None
    for d in range(D1):
        part = sums[d * NCOARSE : (d + 1) * NCOARSE]
        part = shifted([part[:, c * LANES : (c + 1) * LANES] for c in range(NCH)], d, lane)
        totals = part if totals is None else [a + b for a, b in zip(totals, part)]
    for c in range(NCH):
        out_ref[pl.ds(c, NCOARSE, stride=ROW), :] = totals[c]


def fine_kernel(widths_ref, moved_ref, delay_ref, square_ref, peak_ref):
    lane = lane_ids(NSUB)
    raw = [moved_ref[pl.ds(c, NSUB, stride=ROW), :] for c in range(NCH)]
    zero = [
        jnp.broadcast_to(
            jnp.sum(moved_ref[pl.ds(NCH + c, NSUB, stride=ROW), :], axis=0, keepdims=True)
            * (1.0 / C),
            (D1, LANES),
        )
        for c in range(NCH)
    ]
    counts = moved_ref[pl.ds(2 * NCH, NSUB, stride=ROW), :]

    lane8 = lane_ids(D1)
    row8 = lax.broadcasted_iota(jnp.int32, (D1, LANES), 0)
    later = zero
    for d in range(1, D1):
        moved_on = shifted(zero, d, lane8)
        later = [jnp.where(row8 == d, moved_on[c], later[c]) for c in range(NCH)]
    later = jnp.concatenate(later, axis=1)
    parts = [p.astype(jnp.float32) for p in pieces(later, SPLITS)]
    parts.append(jnp.zeros_like(parts[0]))
    zero_rows = jnp.concatenate(parts, axis=0).astype(jnp.bfloat16)
    level = jnp.dot(
        counts[:, : 4 * D1].astype(jnp.bfloat16), zero_rows, preferred_element_type=jnp.float32
    )
    subbands = [raw[c] - level[:, c * LANES : (c + 1) * LANES] for c in range(NCH)]

    delay = delay_ref[...]
    delay4 = jnp.concatenate([delay] * 4, axis=1)
    low = (lax.broadcasted_iota(jnp.int32, (JDEV, 4 * NSUB), 1) // NSUB) % F0
    weights = jnp.concatenate(
        [
            (delay4 == F0 * f + low).astype(jnp.float32).astype(jnp.bfloat16)
            for f in range(F1)
        ],
        axis=0,
    )
    by_lag = [
        pieces(jnp.concatenate(shifted(subbands, f, lane), axis=1), 2) for f in range(F0)
    ]
    data = jnp.concatenate([by_lag[f][s] for s in range(2) for f in range(F0)], axis=0)
    sums = jnp.dot(weights, data, preferred_element_type=jnp.float32)
    lane32 = lane_ids(JDEV)
    series = None
    for f in range(F1):
        part = sums[f * JDEV : (f + 1) * JDEV]
        part = shifted(
            [part[:, c * LANES : (c + 1) * LANES] for c in range(NCH)], F0 * f, lane32
        )
        series = part if series is None else [a + b for a, b in zip(series, part)]

    mean = jnp.sum(sum(series), axis=1, keepdims=True) * (1.0 / S)
    centered = [s - mean for s in series]
    square = jnp.sum(sum(x * x for x in centered))
    square_ref[...] = jnp.broadcast_to(square, square_ref.shape)

    stacked = jnp.concatenate(centered, axis=0)
    both = jnp.concatenate(pieces(stacked, 2), axis=1)
    before = lax.broadcasted_iota(jnp.int32, (2 * LANES, 2 * LANES), 0) % LANES
    column = lax.broadcasted_iota(jnp.int32, (2 * LANES, 2 * LANES), 1)
    ladder = jnp.where(
        jnp.logical_or(before < column, column >= LANES), 1.0, 0.0
    ).astype(jnp.bfloat16)
    sums = jnp.dot(both, ladder, preferred_element_type=jnp.float32)
    prefix = []
    done = jnp.zeros((JDEV, LANES), jnp.float32)
    for c in range(NCH):
        prefix.append(sums[c * JDEV : (c + 1) * JDEV, :LANES] + done)
        done = done + sums[c * JDEV : (c + 1) * JDEV, LANES:]
    peaks = jnp.zeros((JDEV, LANES), jnp.float32)
    for i in range(NW):
        width = widths_ref[i]
        rolled = [pltpu.roll(p, LANES - width, axis=1) for p in prefix] + [done]
        here = lane32 < LANES - width
        best = None
        for c in range(NCH):
            box = jnp.where(here, rolled[c], rolled[c + 1]) - prefix[c]
            best = box if best is None else jnp.maximum(best, box)
        best = jnp.max(best, axis=1, keepdims=True)
        root = lax.rsqrt(jnp.full((JDEV, LANES), width.astype(jnp.float32)))
        peaks = jnp.where(lane32 == i, best * root, peaks)
    peak_ref[...] = peaks


def last_kernel(square_ref, peak_ref, out_ref):
    total = jnp.sum(square_ref[...], axis=0, keepdims=True)
    sigma = jnp.sqrt(total * (1.0 / (NDM * S)) + 1e-06)
    out_ref[...] = (peak_ref[...] / sigma)[:, :NW]


VMEM = pl.BlockSpec(memory_space=pltpu.VMEM)
SMEM = pl.BlockSpec(memory_space=pltpu.SMEM)


def body(spectra, rfi_flags, sub_delay, fine_delay, widths):
    lanes = lax.axis_size("lane")
    seg = lax.axis_index("segment").astype(jnp.int32).reshape(1)
    message = pl.pallas_call(
        front_kernel,
        name="front",
        grid_spec=pltpu.PrefetchScalarGridSpec(
            num_scalar_prefetch=1,
            grid=(1,),
            in_specs=[
                pl.BlockSpec((1, SUBCH, S), lambda i, seg: (seg[0], 0, 0)),
                pl.BlockSpec((1, SUBCH, NCH), lambda i, seg: (seg[0], 0, 0)),
                pl.BlockSpec((NCOARSE, SUBCH), lambda i, seg: (0, 0)),
            ],
            out_specs=pl.BlockSpec((NCOARSE * ROW, LANES), lambda i, seg: (0, 0)),
        ),
        out_shape=jax.ShapeDtypeStruct((NCOARSE * ROW, LANES), jnp.float32),
    )(seg, spectra, rfi_flags, sub_delay)
    moved = lax.all_to_all(
        message.reshape(lanes, 1, ROW * LANES), "lane", split_axis=0, concat_axis=0, tiled=True
    )
    square, peaks = pl.pallas_call(
        fine_kernel,
        name="fine",
        in_specs=[SMEM, VMEM, VMEM],
        out_specs=[VMEM, VMEM],
        out_shape=[
            jax.ShapeDtypeStruct((lanes, LANES), jnp.float32),
            jax.ShapeDtypeStruct((JDEV, LANES), jnp.float32),
        ],
    )(widths, moved.reshape(lanes * ROW, LANES), fine_delay)
    squares = lax.all_to_all(
        square.reshape(lanes, 1, LANES), "lane", split_axis=0, concat_axis=0, tiled=True
    )
    out = pl.pallas_call(
        last_kernel,
        name="last",
        in_specs=[VMEM, VMEM],
        out_specs=VMEM,
        out_shape=jax.ShapeDtypeStruct((JDEV, NW), jnp.float32),
    )(squares.reshape(lanes, LANES), peaks)
    return out[None]


def solution(mesh):
    in_specs = (P(None, "lane", None), P(None, "lane", None), P(None, "lane"), P("lane", None), P())
    out_specs = P("segment", "lane", None)
    return jax.shard_map(body, mesh=mesh, in_specs=in_specs, out_specs=out_specs, check_vma=False)
```

time: 109 us -> 57.9 us (0.53)
  blocking collectives: 0 us -> 46.9 us
  local copies, waits for them, and re-layouts: 34.5 us -> 2.84 us
  starting transfers between devices: 25.2 us -> 0 us
  waiting for transfers between devices: 22.9 us -> 0 us
  other arithmetic: 19.5 us -> 0 us
  Pallas kernels: 0 us -> 7.65 us
  matrix products: 5.24 us -> 0 us
    all_to_all x0 -> x2, blocking collectives: none -> 46.9 us  [the longest x1 31.3 us: body(): lax.all_to_all(message.reshape(lanes, 1, ROW * LANES), 'lane', split_axis...]
    gather x1 -> x0, local copies, waits for them, and re-layouts: 27.7 us -> none  [detect(): upper = prefix[:, ends]]
    all_to_all x3 -> x0, starting transfers between devices: 25.2 us -> none  [the longest x2 19.2 us: sent_to_all(): return lax.all_to_all(copies, axis, split_axis=0, concat_axis=0, tiled=True)]
    all_to_all x3 -> x0, waiting for transfers between devices: 22.9 us -> none  [the longest x1 11.8 us: body(): lax.all_to_all(totals, 'lane', split_axis=0, concat_axis=1, tiled=True)]
    another operation x3 -> x0, other arithmetic: 9.15 us -> none
    pallas_call x0 -> x3, Pallas kernels: none -> 7.65 us  [the longest x1 3.41 us: body(): pl.pallas_call(fine_kernel, name='fine', in_specs=[SMEM, VMEM, VMEM], out...]
    dot_general x10 -> x0, matrix products: 5.24 us -> none  [the longest x8 4.15 us: fine_sums(): jnp.einsum('gjx,gxs->gjs', weights, stacked, precision=lax.Precision.HIGH...]
    reduce_sum x6 -> x0, other arithmetic: 4.86 us -> none  [the longest x1 1.15 us: clean_block(): jnp.mean((masked - centre) * (masked - centre), axis=1, keepdims=True)]
  transfers between devices with their start and end apart: 3 -> 0, of which waited for: 2 -> 0; matrix products, arithmetic and copies ran while one was open for 27% -> 0% of each run, Pallas kernels for 0% -> 0%
where the time goes in v1:
time: 57.9 us; the launch traced here: 57.4 us
  blocking collectives  46.9 us (81%)
  Pallas kernels  7.65 us (13%)
  local copies, waits for them, and re-layouts  2.84 us (5%)
    all_to_all x1, blocking collectives, body(): lax.all_to_all(message.reshape(lanes, 1, ROW * LANES), 'lane', split_axis...  31.3 us
    all_to_all x1, blocking collectives, body(): lax.all_to_all(square.reshape(lanes, 1, LANES), 'lane', split_axis=0, con...  15.7 us
    pallas_call x1, Pallas kernels, body(): pl.pallas_call(fine_kernel, name='fine', in_specs=[SMEM, VMEM, VMEM], out...  3.41 us
    pallas_call x1, Pallas kernels, body(): pl.pallas_call(front_kernel, name='front', grid_spec=pltpu.PrefetchScalar...  2.84 us
    unnamed x1, local copies, waits for them, and re-layouts  1.47 us
    pallas_call x1, Pallas kernels, body(): pl.pallas_call(last_kernel, name='last', in_specs=[VMEM, VMEM], out_specs...  1.39 us
    broadcast_in_dim x1, local copies, waits for them, and re-layouts, body(): return out[None]  1.38 us

profile of v1, /device:TPU:1, one launch (start us, length us, event | category | flops | bytes accessed | tf_op | source)
XLA Modules:
  0.0 57.4 jit_solution(13158361781660453307)
XLA Ops:
  0.0 1.5 %copy.8.flags_ref = s32[4,64,8]{2,1,0:T(8,128)} copy(s32[4,64,8]{1,2,0:T(8,128)} %param.6) | data formatting | bytes 16384 | tf_op args[1]
  1.5 2.8 %front.1 = f32[1088,128]{1,0:T(8,128)} custom-call(s32[1]{0:T(128)} %bitcast.seg_ref, f32[4,64,1024]{2,1,0:T(8,128)} %power_ref.1, s32[4,64,8]{2,1,0:T(8,128)} %copy.8.flags_ref, s32[64,64]{1,0:T(8,128)} %delay_ref.2), custom_call_target="tpu_custom_call" | custom-call | tf_op jit(solution)/shard_map/front/pallas_call | solution.py:195
  4.3 31.3 %all_to_all.10 = f32[64,1,2176]{2,1,0:T(1,128)} all-to-all(f32[64,1,2176]{2,1,0:T(1,128)} %bitcast.9), channel_id=1, replica_groups=mesh['segment'=4,'lane'=64] {'lane'}, dimensions={0} | all-to-all | bytes 1114112 | tf_op jit(solution)/shard_map/all_to_all | solution.py:210
  35.6 3.4 %fine.1 = (f32[64,128]{1,0:T(8,128)}, f32[32,128]{1,0:T(8,128)}) custom-call(s32[8]{0:T(128)} %widths_ref.1, f32[1088,128]{1,0:T(8,128)} %bitcast.8, s32[32,64]{1,0:T(8,128)} %delay_ref.3), custom_call_target="tpu_custom_call" | custom-call | tf_op jit(solution)/shard_map/fine/pallas_call | solution.py:213
  39.0 15.7 %all_to_all.11 = f32[64,1,128]{2,1,0:T(1,128)} all-to-all(f32[64,1,128]{2,1,0:T(1,128)} %bitcast.12), channel_id=1, replica_groups=mesh['segment'=4,'lane'=64] {'lane'}, dimensions={0} | all-to-all | bytes 65536 | tf_op jit(solution)/shard_map/all_to_all | solution.py:223
  54.7 1.4 %last.1 = f32[32,8]{1,0:T(8,128)} custom-call(f32[64,128]{1,0:T(8,128)} %bitcast.10, f32[32,128]{1,0:T(8,128)} %get-tuple-element.8.peak_ref), custom_call_target="tpu_custom_call" | custom-call | tf_op jit(solution)/shard_map/last/pallas_call | solution.py:226
  56.1 1.4 %copy.11 = f32[1,32,8]{1,2,0:T(8,128)} copy(f32[1,32,8]{2,1,0:T(8,128)} %bitcast.11) | data formatting | bytes 2048 | tf_op jit(solution)/shard_map/broadcast_in_dim | solution.py:233

commit v2 on v1

--- a/solution.py
+++ b/solution.py
@@ -46,24 +46,17 @@
     return parts
 
 
-def front_kernel(seg_ref, power_ref, flags_ref, delay_ref, out_ref):
-    del seg_ref
-    keep = 1.0 - flags_ref[0].astype(jnp.float32)
-    kept = [jnp.broadcast_to(keep[:, c : c + 1], (SUBCH, LANES)) for c in range(NCH)]
-    power = [power_ref[0, :, c * LANES : (c + 1) * LANES] for c in range(NCH)]
-    masked = [kept[c] * power[c] for c in range(NCH)]
-    centre = jnp.sum(sum(masked), axis=1, keepdims=True) * (1.0 / S)
-    spread = sum((m - centre) * (m - centre) for m in masked)
-    spread = jnp.sum(spread, axis=1, keepdims=True) * (1.0 / S)
-    scale = lax.rsqrt(spread + 1e-05)
-    normed = [kept[c] * (power[c] - centre) * scale for c in range(NCH)]
-
-    for c in range(NCH):
-        channel_sum = jnp.sum(normed[c], axis=0, keepdims=True)
-        out_ref[pl.ds(NCH + c, NCOARSE, stride=ROW), :] = jnp.broadcast_to(
-            channel_sum, (NCOARSE, LANES)
-        )
-
+def front_kernel(power_hbm, flags_hbm, delay_hbm, out_ref, power_ref, flags_ref, delay_ref, sems):
+    mine = lax.axis_index("segment")
+    copies = [
+        pltpu.make_async_copy(delay_hbm, delay_ref, sems.at[0]),
+        pltpu.make_async_copy(flags_hbm.at[mine], flags_ref, sems.at[1]),
+        pltpu.make_async_copy(power_hbm.at[mine], power_ref, sems.at[2]),
+    ]
+    for copy in copies:
+        copy.start()
+
+    copies[0].wait()
     delay = delay_ref[...]
     lane = lane_ids(NCOARSE)
     counts = jnp.zeros((NCOARSE, LANES), jnp.float32)
@@ -73,11 +66,37 @@
             jnp.logical_and(lane % D1 == d, lane < SPLITS * D1), count, counts
         )
     out_ref[pl.ds(2 * NCH, NCOARSE, stride=ROW), :] = counts
-
     delay4 = jnp.concatenate([delay] * 4, axis=1)
     weights = jnp.concatenate(
         [(delay4 == d).astype(jnp.float32).astype(jnp.bfloat16) for d in range(D1)], axis=0
     )
+
+    copies[1].wait()
+    copies[2].wait()
+    keep = (1.0 - flags_ref[...].astype(jnp.float32)).astype(jnp.bfloat16)
+    block = lax.broadcasted_iota(jnp.int32, (NCH, S), 1) // LANES
+    own = block == lax.broadcasted_iota(jnp.int32, (NCH, S), 0)
+    kept = lax.dot_general(
+        keep,
+        own.astype(jnp.float32).astype(jnp.bfloat16),
+        (((0,), (0,)), ((), ())),
+        preferred_element_type=jnp.float32,
+    )
+    kept = [kept[:, c * LANES : (c + 1) * LANES] for c in range(NCH)]
+    power = [power_ref[:, c * LANES : (c + 1) * LANES] for c in range(NCH)]
+    masked = [kept[c] * power[c] for c in range(NCH)]
+    centre = jnp.sum(sum(masked), axis=1, keepdims=True) * (1.0 / S)
+    spread = sum((m - centre) * (m - centre) for m in masked)
+    spread = jnp.sum(spread, axis=1, keepdims=True) * (1.0 / S)
+    scale = lax.rsqrt(spread + 1e-05)
+    normed = [kept[c] * (power[c] - centre) * scale for c in range(NCH)]
+
+    for c in range(NCH):
+        channel_sum = jnp.sum(normed[c], axis=0, keepdims=True)
+        out_ref[pl.ds(NCH + c, NCOARSE, stride=ROW), :] = jnp.broadcast_to(
+            channel_sum, (NCOARSE, LANES)
+        )
+
     split = [pieces(n, SPLITS) for n in normed]
     rows = [
         jnp.concatenate([split[c][s] for c in range(NCH)], axis=1) for s in range(SPLITS)
@@ -94,7 +113,9 @@
         out_ref[pl.ds(c, NCOARSE, stride=ROW), :] = totals[c]
 
 
-def fine_kernel(widths_ref, moved_ref, delay_ref, square_ref, peak_ref):
+def fine_kernel(widths_hbm, moved_ref, delay_ref, square_ref, peak_ref, widths_ref, sem):
+    fetch = pltpu.make_async_copy(widths_hbm, widths_ref, sem)
+    fetch.start()
     lane = lane_ids(NSUB)
     raw = [moved_ref[pl.ds(c, NSUB, stride=ROW), :] for c in range(NCH)]
     zero = [
@@ -165,6 +186,7 @@
         prefix.append(sums[c * JDEV : (c + 1) * JDEV, :LANES] + done)
         done = done + sums[c * JDEV : (c + 1) * JDEV, LANES:]
     peaks = jnp.zeros((JDEV, LANES), jnp.float32)
+    fetch.wait()
     for i in range(NW):
         width = widths_ref[i]
         rolled = [pltpu.roll(p, LANES - width, axis=1) for p in prefix] + [done]
@@ -176,50 +198,59 @@
         best = jnp.max(best, axis=1, keepdims=True)
         root = lax.rsqrt(jnp.full((JDEV, LANES), width.astype(jnp.float32)))
         peaks = jnp.where(lane32 == i, best * root, peaks)
-    peak_ref[...] = peaks
+    peak_ref[...] = peaks.T[:NW]
 
 
 def last_kernel(square_ref, peak_ref, out_ref):
     total = jnp.sum(square_ref[...], axis=0, keepdims=True)
     sigma = jnp.sqrt(total * (1.0 / (NDM * S)) + 1e-06)
-    out_ref[...] = (peak_ref[...] / sigma)[:, :NW]
+    out_ref[...] = peak_ref[...] / sigma[:, :JDEV]
 
 
 VMEM = pl.BlockSpec(memory_space=pltpu.VMEM)
-SMEM = pl.BlockSpec(memory_space=pltpu.SMEM)
+ANY = pl.BlockSpec(memory_space=pl.ANY)
+PARAMS = pltpu.CompilerParams(vmem_limit_bytes=32 * 1024 * 1024)
+
+
+def in_hbm(x):
+    return pltpu.with_memory_space_constraint(x, pltpu.HBM)
+
+
+def in_vmem(x):
+    return pltpu.with_memory_space_constraint(x, pltpu.VMEM)
 
 
 def body(spectra, rfi_flags, sub_delay, fine_delay, widths):
     lanes = lax.axis_size("lane")
-    seg = lax.axis_index("segment").astype(jnp.int32).reshape(1)
     message = pl.pallas_call(
         front_kernel,
         name="front",
-        grid_spec=pltpu.PrefetchScalarGridSpec(
-            num_scalar_prefetch=1,
-            grid=(1,),
-            in_specs=[
-                pl.BlockSpec((1, SUBCH, S), lambda i, seg: (seg[0], 0, 0)),
-                pl.BlockSpec((1, SUBCH, NCH), lambda i, seg: (seg[0], 0, 0)),
-                pl.BlockSpec((NCOARSE, SUBCH), lambda i, seg: (0, 0)),
-            ],
-            out_specs=pl.BlockSpec((NCOARSE * ROW, LANES), lambda i, seg: (0, 0)),
-        ),
-        out_shape=jax.ShapeDtypeStruct((NCOARSE * ROW, LANES), jnp.float32),
-    )(seg, spectra, rfi_flags, sub_delay)
+        in_specs=[ANY, ANY, ANY],
+        out_specs=VMEM,
+        out_shape=pltpu.VMEM((NCOARSE * ROW, LANES), jnp.float32),
+        scratch_shapes=[
+            pltpu.VMEM((SUBCH, S), jnp.float32),
+            pltpu.VMEM((NCH, SUBCH), jnp.int32),
+            pltpu.VMEM((NCOARSE, SUBCH), jnp.int32),
+            pltpu.SemaphoreType.DMA((3,)),
+        ],
+        compiler_params=PARAMS,
+    )(in_hbm(spectra), in_hbm(jnp.transpose(rfi_flags, (0, 2, 1))), in_hbm(sub_delay))
     moved = lax.all_to_all(
         message.reshape(lanes, 1, ROW * LANES), "lane", split_axis=0, concat_axis=0, tiled=True
     )
     square, peaks = pl.pallas_call(
         fine_kernel,
         name="fine",
-        in_specs=[SMEM, VMEM, VMEM],
+        in_specs=[ANY, VMEM, VMEM],
         out_specs=[VMEM, VMEM],
         out_shape=[
-            jax.ShapeDtypeStruct((lanes, LANES), jnp.float32),
-            jax.ShapeDtypeStruct((JDEV, LANES), jnp.float32),
+            pltpu.VMEM((lanes, LANES), jnp.float32),
+            pltpu.VMEM((NW, JDEV), jnp.float32),
         ],
-    )(widths, moved.reshape(lanes * ROW, LANES), fine_delay)
+        scratch_shapes=[pltpu.SMEM((NW,), jnp.int32), pltpu.SemaphoreType.DMA],
+        compiler_params=PARAMS,
+    )(in_hbm(widths), in_vmem(moved.reshape(lanes * ROW, LANES)), fine_delay)
     squares = lax.all_to_all(
         square.reshape(lanes, 1, LANES), "lane", split_axis=0, concat_axis=0, tiled=True
     )
@@ -228,9 +259,10 @@
         name="last",
         in_specs=[VMEM, VMEM],
         out_specs=VMEM,
-        out_shape=jax.ShapeDtypeStruct((JDEV, NW), jnp.float32),
-    )(squares.reshape(lanes, LANES), peaks)
-    return out[None]
+        out_shape=jax.ShapeDtypeStruct((NW, JDEV), jnp.float32),
+        compiler_params=PARAMS,
+    )(in_vmem(squares.reshape(lanes, LANES)), peaks)
+    return out.T[None]
 
 
 def solution(mesh):

time: 57.9 us -> 51.8 us (0.89)
  local copies, waits for them, and re-layouts: 2.84 us -> 0.01 us
  Pallas kernels: 7.65 us -> 5.25 us
  blocking collectives: 46.9 us -> 46.3 us
    pallas_call x2, Pallas kernels: 6.26 us -> 4.63 us  [the longest x1 2.48 us: body(): pl.pallas_call(fine_kernel, name='fine', in_specs=[ANY, VMEM, VMEM], out_...]
    unnamed x1 -> x2, local copies, waits for them, and re-layouts: 1.47 us -> 0.01 us
    broadcast_in_dim x1 -> x0, local copies, waits for them, and re-layouts: 1.38 us -> none  [body(): return out[None]]
    pallas_call x1, Pallas kernels: 1.39 us -> 0.62 us  [body(): pl.pallas_call(last_kernel, name='last', in_specs=[VMEM, VMEM], out_specs...]
where the time goes in v2:
time: 51.8 us; the launch traced here: 51.6 us
  blocking collectives  46.3 us (89%)
  Pallas kernels  5.25 us (10%)
    all_to_all x1, blocking collectives, body(): lax.all_to_all(message.reshape(lanes, 1, ROW * LANES), 'lane', split_axis...  31 us
    all_to_all x1, blocking collectives, body(): lax.all_to_all(square.reshape(lanes, 1, LANES), 'lane', split_axis=0, con...  15.4 us
    pallas_call x1, Pallas kernels, body(): pl.pallas_call(fine_kernel, name='fine', in_specs=[ANY, VMEM, VMEM], out_...  2.48 us
    pallas_call x1, Pallas kernels, body(): pl.pallas_call(front_kernel, name='front', in_specs=[ANY, ANY, ANY], out_...  2.15 us

profile of v2, /device:TPU:1, one launch (start us, length us, event | category | flops | bytes accessed | tf_op | source)
XLA Modules:
  0.0 51.6 jit_solution(16163137871775329871)
XLA Ops:
  0.0 2.2 %front.1 = f32[1088,128]{1,0:T(8,128)S(1)} custom-call(f32[4,64,1024]{2,1,0:T(8,128)} %power_hbm.1, s32[4,8,64]{2,1,0:T(8,128)} %bitcast.14, s32[64,64]{1,0:T(8,128)} %delay_hbm.1), custom_call_target="tpu_custom_call" | custom-call | tf_op jit(solution)/shard_map/front/pallas_call | solution.py:225
  2.2 0.0 copy-start
  2.2 31.0 %all_to_all.10 = f32[64,1,2176]{2,1,0:T(1,128)S(1)} all-to-all(f32[64,1,2176]{2,1,0:T(1,128)S(1)} %bitcast.11), channel_id=1, replica_groups=mesh['segment'=4,'lane'=64] {'lane'}, dimensions={0} | all-to-all | bytes 1114112 | tf_op jit(solution)/shard_map/all_to_all | solution.py:239
  33.1 0.0 copy-done
  33.2 2.5 %fine.1 = (f32[64,128]{1,0:T(8,128)S(1)}, f32[8,32]{1,0:T(8,128)S(1)}) custom-call(s32[8]{0:T(128)} %widths_hbm.1, f32[1088,128]{1,0:T(8,128)S(1)} %bitcast.10, s32[32,64]{1,0:T(8,128)S(1)} %copy-done), custom_call_target="tpu_custom_call" | custom-call | tf_op jit(solution)/shard_map/fine/pallas_call | solution.py:242
  35.6 15.4 %all_to_all.11 = f32[64,1,128]{2,1,0:T(1,128)S(1)} all-to-all(f32[64,1,128]{2,1,0:T(1,128)S(1)} %bitcast.13), channel_id=1, replica_groups=mesh['segment'=4,'lane'=64] {'lane'}, dimensions={0} | all-to-all | bytes 65536 | tf_op jit(solution)/shard_map/all_to_all | solution.py:254
  51.0 0.6 %last.1 = f32[8,32]{1,0:T(8,128)} custom-call(f32[64,128]{1,0:T(8,128)S(1)} %bitcast.12, f32[8,32]{1,0:T(8,128)S(1)} %get-tuple-element.8.peak_ref), custom_call_target="tpu_custom_call" | custom-call | tf_op jit(solution)/shard_map/last/pallas_call | solution.py:257
Async XLA Ops:
  2.2 31.0 %copy-start = (s32[32,64]{1,0:T(8,128)S(1)}, s32[32,64]{1,0:T(8,128)}, u32[]{:S(2)}) copy-start(s32[32,64]{1,0:T(8,128)} %delay_ref.1) | copy-start | bytes 24580

commit v3 on v2

v3 whole, which is shorter than its diff:
```python
import jax
import jax.numpy as jnp
from jax import lax
from jax.experimental import pallas as pl
from jax.experimental.pallas import tpu as pltpu
from jax.sharding import PartitionSpec as P

C = 4096
SUBCH = 64
NSUB = 64
NCOARSE = 64
NDM = 2048
S = 1024
D1 = 8
D2 = 32
NW = 8
WMAX = 64
GAP = 2
JDEV = 32
LANES = 128
NCH = S // LANES
ROW = 2 * NCH + 1
SPLITS = 3
FINE_SPLITS = 2
ORDER = (37, 11, 21)


def peer(i):
    i = (i * ORDER[0] + ORDER[1]) & 63
    i = i ^ (i >> 3)
    i = (i * ORDER[2]) & 63
    return i ^ (i >> 2)


def lane_ids(rows):
    return lax.broadcasted_iota(jnp.int32, (rows, LANES), 1)


def shifted(chunks, amount, lane):
    if amount == 0:
        return chunks
    rolled = [pltpu.roll(c, LANES - amount, axis=1) for c in chunks]
    rolled.append(jnp.zeros_like(rolled[0]))
    return [
        jnp.where(lane < LANES - amount, rolled[c], rolled[c + 1]) for c in range(len(chunks))
    ]


def pieces(x, count):
    parts = []
    for _ in range(count):
        part = x.astype(jnp.bfloat16)
        parts.append(part)
        x = x - part.astype(jnp.float32)
    return parts


def lag_rows(chunks, lags, count, lane):
    by_lag = [pieces(jnp.concatenate(shifted(chunks, f, lane), axis=1), count) for f in range(lags)]
    return jnp.concatenate([by_lag[f][s] for s in range(count) for f in range(lags)], axis=0)


def selector(shape, axis):
    place = lax.broadcasted_iota(jnp.int32, shape, axis) % 64
    lane = lax.broadcasted_iota(jnp.int32, shape, 1 - axis)
    return (lane == peer(place)).astype(jnp.float32).astype(jnp.bfloat16)


def small(delay):
    return delay.astype(jnp.float32).astype(jnp.bfloat16)


def one_hot(wide, width, groups):
    lag = (lax.broadcasted_iota(jnp.int32, wide.shape, 1) // width) % 2
    wide = wide - lag.astype(jnp.float32)
    return jnp.concatenate(
        [(wide == 2.0 * g).astype(jnp.float32).astype(jnp.bfloat16) for g in range(groups)],
        axis=0,
    )


def front_kernel(
    power_hbm, flags_hbm, delay_hbm, widths_hbm, out_ref, widths_ref, power_ref, flags_ref, delay_ref, sems
):
    mine = lax.axis_index("segment")
    widths_copy = pltpu.make_async_copy(widths_hbm, widths_ref, sems.at[3])
    copies = [
        pltpu.make_async_copy(delay_hbm, delay_ref, sems.at[0]),
        pltpu.make_async_copy(flags_hbm.at[mine], flags_ref, sems.at[1]),
        pltpu.make_async_copy(power_hbm.at[mine], power_ref, sems.at[2]),
    ]
    for copy in copies:
        copy.start()
    widths_copy.start()

    copies[0].wait()
    delay = jnp.dot(
        selector((NCOARSE, NCOARSE), 0),
        small(delay_ref[...]),
        preferred_element_type=jnp.float32,
    )
    lane = lane_ids(NCOARSE)
    counts = jnp.zeros((NCOARSE, LANES), jnp.float32)
    for d in range(D1):
        count = jnp.sum((delay == float(d)).astype(jnp.float32), axis=1, keepdims=True)
        counts = jnp.where(
            jnp.logical_and(lane % D1 == d, lane < SPLITS * D1), count, counts
        )
    out_ref[pl.ds(2 * NCH, NCOARSE, stride=ROW), :] = counts
    weights = one_hot(jnp.concatenate([delay] * (2 * SPLITS), axis=1), SUBCH, D1 // 2)

    copies[1].wait()
    keep = (1.0 - flags_ref[...].astype(jnp.float32)).astype(jnp.bfloat16)
    block = lax.broadcasted_iota(jnp.int32, (NCH, S), 1) // LANES
    own = block == lax.broadcasted_iota(jnp.int32, (NCH, S), 0)
    kept = lax.dot_general(
        keep,
        own.astype(jnp.float32).astype(jnp.bfloat16),
        (((0,), (0,)), ((), ())),
        preferred_element_type=jnp.float32,
    )
    kept = [kept[:, c * LANES : (c + 1) * LANES] for c in range(NCH)]
    copies[2].wait()
    power = [power_ref[:, c * LANES : (c + 1) * LANES] for c in range(NCH)]
    masked = [kept[c] * power[c] for c in range(NCH)]
    centre = jnp.sum(sum(masked), axis=1, keepdims=True) * (1.0 / S)
    spread = sum((m - centre) * (m - centre) for m in masked)
    spread = jnp.sum(spread, axis=1, keepdims=True) * (1.0 / S)
    scale = lax.rsqrt(spread + 1e-05)
    normed = [kept[c] * (power[c] - centre) * scale for c in range(NCH)]

    for c in range(NCH):
        channel_sum = jnp.sum(normed[c], axis=0, keepdims=True)
        out_ref[pl.ds(NCH + c, NCOARSE, stride=ROW), :] = jnp.broadcast_to(
            channel_sum, (NCOARSE, LANES)
        )

    data = lag_rows(normed, 2, SPLITS, lane)
    sums = jnp.dot(weights, data, preferred_element_type=jnp.float32)
    totals = None
    for d in range(D1 // 2):
        part = sums[d * NCOARSE : (d + 1) * NCOARSE]
        part = shifted([part[:, c * LANES : (c + 1) * LANES] for c in range(NCH)], 2 * d, lane)
        totals = part if totals is None else [a + b for a, b in zip(totals, part)]
    for c in range(NCH):
        out_ref[pl.ds(c, NCOARSE, stride=ROW), :] = totals[c]
    widths_copy.wait()


def fine_kernel(widths_ref, moved_ref, delay_ref, square_ref, peak_ref, ramp_ref):
    lane = lane_ids(NSUB)
    raw = [moved_ref[pl.ds(c, NSUB, stride=ROW), :] for c in range(NCH)]
    zero = [
        jnp.broadcast_to(
            jnp.sum(moved_ref[pl.ds(NCH + c, NSUB, stride=ROW), :], axis=0, keepdims=True)
            * (1.0 / C),
            (D1, LANES),
        )
        for c in range(NCH)
    ]
    counts = moved_ref[pl.ds(2 * NCH, NSUB, stride=ROW), :]

    lane8 = lane_ids(D1)
    row8 = lax.broadcasted_iota(jnp.int32, (D1, LANES), 0)
    later = zero
    for d in range(1, D1):
        moved_on = shifted(zero, d, lane8)
        later = [jnp.where(row8 == d, moved_on[c], later[c]) for c in range(NCH)]
    later = jnp.concatenate(later, axis=1)
    parts = [p.astype(jnp.float32) for p in pieces(later, SPLITS)]
    parts.append(jnp.zeros_like(parts[0]))
    zero_rows = jnp.concatenate(parts, axis=0).astype(jnp.bfloat16)
    level = jnp.dot(
        counts[:, : 4 * D1].astype(jnp.bfloat16), zero_rows, preferred_element_type=jnp.float32
    )
    subbands = [raw[c] - level[:, c * LANES : (c + 1) * LANES] for c in range(NCH)]

    wide = jnp.dot(
        small(delay_ref[...]),
        selector((NSUB, 2 * FINE_SPLITS * NSUB), 1),
        preferred_element_type=jnp.float32,
    )
    weights = one_hot(wide, NSUB, D2 // 2)
    data = lag_rows(subbands, 2, FINE_SPLITS, lane)
    sums = jnp.dot(weights, data, preferred_element_type=jnp.float32)
    lane32 = lane_ids(JDEV)
    series = None
    for f in range(D2 // 2):
        part = sums[f * JDEV : (f + 1) * JDEV]
        part = shifted(
            [part[:, c * LANES : (c + 1) * LANES] for c in range(NCH)], 2 * f, lane32
        )
        series = part if series is None else [a + b for a, b in zip(series, part)]

    mean = jnp.sum(sum(series), axis=1, keepdims=True) * (1.0 / S)
    centered = [s - mean for s in series]
    square = jnp.sum(sum(x * x for x in centered))
    square_ref[...] = jnp.broadcast_to(square, square_ref.shape)

    half = NCH // 2
    across = jnp.concatenate(
        [jnp.concatenate(centered[h * half : (h + 1) * half], axis=0).T for h in range(2)], axis=1
    )
    data = jnp.concatenate(pieces(across, FINE_SPLITS), axis=0)
    shape = (LANES + 8, FINE_SPLITS * LANES)
    ladder = lax.broadcasted_iota(jnp.int32, shape, 1) % LANES < lax.broadcasted_iota(
        jnp.int32, shape, 0
    )
    ramp = jnp.dot(
        ladder.astype(jnp.float32).astype(jnp.bfloat16), data, preferred_element_type=jnp.float32
    )
    lane = lane_ids(WMAX)
    total = jnp.broadcast_to(ramp[LANES : LANES + 1], (WMAX, 2 * LANES))
    first = pltpu.roll(ramp[:WMAX, :LANES], LANES - JDEV, axis=1)
    second = pltpu.roll(ramp[:WMAX, LANES:], LANES - JDEV, axis=1)
    follow = lane < LANES - JDEV
    low = [ramp[:LANES, :LANES], ramp[:LANES, LANES:]]
    high = [
        total[:, :LANES] + jnp.where(follow, first, second),
        total[:, LANES:] + jnp.where(follow, second, 0.0),
    ]
    for h in range(2):
        ramp_ref[h, pl.ds(0, LANES, stride=GAP), :] = low[h]
        ramp_ref[h, pl.ds(GAP * LANES, WMAX, stride=GAP), :] = high[h]
    row8 = lax.broadcasted_iota(jnp.int32, (NW, 2 * LANES), 0)
    peaks = jnp.zeros((NW, 2 * LANES), jnp.float32)
    for i in range(NW):
        width = widths_ref[i]
        best = [
            jnp.max(ramp_ref[h, pl.ds(GAP * width, LANES, stride=GAP), :] - low[h], axis=0, keepdims=True)
            for h in range(2)
        ]
        best = jnp.concatenate(best, axis=1)
        root = lax.rsqrt(jnp.full((1, 2 * LANES), width.astype(jnp.float32)))
        peaks = jnp.where(row8 == i, best * root, peaks)
    best = jnp.maximum(peaks[:, :LANES], peaks[:, LANES:])
    best = jnp.maximum(best, pltpu.roll(best, 2 * JDEV, axis=1))
    best = jnp.maximum(best, pltpu.roll(best, JDEV, axis=1))
    peak_ref[...] = best[:, :JDEV]


def last_kernel(square_ref, peak_ref, out_ref):
    total = jnp.sum(square_ref[...], axis=0, keepdims=True)
    sigma = jnp.sqrt(total * (1.0 / (NDM * S)) + 1e-06)
    out_ref[...] = peak_ref[...] / sigma[:, :JDEV]


GROUP = [[peer(i) for i in range(NCOARSE)]]
VMEM = pl.BlockSpec(memory_space=pltpu.VMEM)
SMEM = pl.BlockSpec(memory_space=pltpu.SMEM)
ANY = pl.BlockSpec(memory_space=pl.ANY)
PARAMS = pltpu.CompilerParams(vmem_limit_bytes=32 * 1024 * 1024)


def in_hbm(x):
    return pltpu.with_memory_space_constraint(x, pltpu.HBM)


def in_vmem(x):
    return pltpu.with_memory_space_constraint(x, pltpu.VMEM)


def body(spectra, rfi_flags, sub_delay, fine_delay, widths):
    lanes = lax.axis_size("lane")
    message, widths = pl.pallas_call(
        front_kernel,
        name="front",
        in_specs=[ANY, ANY, ANY, ANY],
        out_specs=[VMEM, SMEM],
        out_shape=[
            pltpu.VMEM((NCOARSE * ROW, LANES), jnp.float32),
            pltpu.SMEM((NW,), jnp.int32),
        ],
        scratch_shapes=[
            pltpu.VMEM((SUBCH, S), jnp.float32),
            pltpu.VMEM((NCH, SUBCH), jnp.int32),
            pltpu.VMEM((NCOARSE, SUBCH), jnp.int32),
            pltpu.SemaphoreType.DMA((4,)),
        ],
        compiler_params=PARAMS,
    )(in_hbm(spectra), in_hbm(jnp.transpose(rfi_flags, (0, 2, 1))), in_hbm(sub_delay), in_hbm(widths))
    moved = lax.all_to_all(
        message.reshape(lanes, 1, ROW * LANES), "lane", split_axis=0, concat_axis=0, tiled=True, axis_index_groups=GROUP
    )
    square, peaks = pl.pallas_call(
        fine_kernel,
        name="fine",
        in_specs=[SMEM, VMEM, VMEM],
        out_specs=[VMEM, VMEM],
        out_shape=[
            pltpu.VMEM((lanes, LANES), jnp.float32),
            pltpu.VMEM((NW, JDEV), jnp.float32),
        ],
        scratch_shapes=[pltpu.VMEM((2, GAP * (LANES + WMAX), LANES), jnp.float32)],
        compiler_params=PARAMS,
    )(pltpu.with_memory_space_constraint(widths, pltpu.SMEM), in_vmem(moved.reshape(lanes * ROW, LANES)), fine_delay)
    squares = lax.all_to_all(
        square.reshape(lanes, 1, LANES), "lane", split_axis=0, concat_axis=0, tiled=True, axis_index_groups=GROUP
    )
    out = pl.pallas_call(
        last_kernel,
        name="last",
        in_specs=[VMEM, VMEM],
        out_specs=VMEM,
        out_shape=jax.ShapeDtypeStruct((NW, JDEV), jnp.float32),
        compiler_params=PARAMS,
    )(in_vmem(squares.reshape(lanes, LANES)), peaks)
    return out.T[None]


def solution(mesh):
    in_specs = (P(None, "lane", None), P(None, "lane", None), P(None, "lane"), P("lane", None), P())
    out_specs = P("segment", "lane", None)
    return jax.shard_map(body, mesh=mesh, in_specs=in_specs, out_specs=out_specs, check_vma=False)
```

time: 51.8 us -> 49.8 us (0.961)
  blocking collectives: 46.3 us -> 45 us
  Pallas kernels: 5.25 us -> 4.58 us
    all_to_all x1, blocking collectives: 15.4 us -> 14.4 us  [body(): lax.all_to_all(square.reshape(lanes, 1, LANES), 'lane', split_axis=0, con...]
    pallas_call x2, Pallas kernels: 4.63 us -> 3.96 us  [the longest x1 2.19 us: body(): pl.pallas_call(front_kernel, name='front', in_specs=[ANY, ANY, ANY, ANY],...]
where the time goes in v3:
time: 49.8 us; the launch traced here: 49.6 us
  blocking collectives  45 us (90%)
  Pallas kernels  4.58 us (9%)
    all_to_all x1, blocking collectives, body(): lax.all_to_all(message.reshape(lanes, 1, ROW * LANES), 'lane', split_axis...  30.6 us
    all_to_all x1, blocking collectives, body(): lax.all_to_all(square.reshape(lanes, 1, LANES), 'lane', split_axis=0, con...  14.4 us
    pallas_call x1, Pallas kernels, body(): pl.pallas_call(front_kernel, name='front', in_specs=[ANY, ANY, ANY, ANY],...  2.19 us
    pallas_call x1, Pallas kernels, body(): pl.pallas_call(fine_kernel, name='fine', in_specs=[SMEM, VMEM, VMEM], out...  1.77 us

profile of v3, /device:TPU:1, one launch (start us, length us, event | category | flops | bytes accessed | tf_op | source)
XLA Modules:
  0.0 49.6 jit_solution(16792527976711326097)
XLA Ops:
  0.0 2.2 %front.1 = (f32[1088,128]{1,0:T(8,128)S(1)}, s32[8]{0:T(128)S(4)}) custom-call(f32[4,64,1024]{2,1,0:T(8,128)} %power_hbm.1, s32[4,8,64]{2,1,0:T(8,128)} %bitcast.14, s32[64,64]{1,0:T(8,128)} %delay_hbm.1, s32[8]{0:T(128)} %widths_hbm.1), custom_call_target="tpu_custom_call" | custom-call | tf_op jit(solution)/shard_map/front/pallas_call | solution.py:265
  2.2 0.0 copy-start
  2.2 30.6 %all_to_all.10 = f32[64,1,2176]{2,1,0:T(1,128)S(1)} all-to-all(f32[64,1,2176]{2,1,0:T(1,128)S(1)} %bitcast.11), channel_id=1, replica_groups={{22,37,43,1,15,17,27,53,31,58,2,25,23,26,12,60,54,0,56,46,62,13,19,41,4..., dimensions={0} | all-to-all | bytes 1114112 | tf_op jit(solution)/shard_map/all_to_all | solution.py:282
  32.8 0.0 copy-done
  32.8 1.8 %fine.1 = (f32[64,128]{1,0:T(8,128)S(1)}, f32[8,32]{1,0:T(8,128)S(1)}) custom-call(s32[8]{0:T(128)S(4)} %get-tuple-element.9.widths_ref, f32[1088,128]{1,0:T(8,128)S(1)} %bitcast.10, s32[32,64]{1,0:T(8,128)S(1)} %copy-done), custom_call_target="tpu_custom_call" | custom-call | tf_op jit(solution)/shard_map/fine/pallas_call | solution.py:285
  34.6 14.4 %all_to_all.11 = f32[64,1,128]{2,1,0:T(1,128)S(1)} all-to-all(f32[64,1,128]{2,1,0:T(1,128)S(1)} %bitcast.13), channel_id=1, replica_groups={{22,37,43,1,15,17,27,53,31,58,2,25,23,26,12,60,54,0,56,46,62,13,19,41,4..., dimensions={0} | all-to-all | bytes 65536 | tf_op jit(solution)/shard_map/all_to_all | solution.py:297
  48.9 0.6 %last.1 = f32[8,32]{1,0:T(8,128)} custom-call(f32[64,128]{1,0:T(8,128)S(1)} %bitcast.12, f32[8,32]{1,0:T(8,128)S(1)} %get-tuple-element.12.peak_ref), custom_call_target="tpu_custom_call" | custom-call | tf_op jit(solution)/shard_map/last/pallas_call | solution.py:300
Async XLA Ops:
  2.2 30.6 %copy-start = (s32[32,64]{1,0:T(8,128)S(1)}, s32[32,64]{1,0:T(8,128)}, u32[]{:S(2)}) copy-start(s32[32,64]{1,0:T(8,128)} %delay_ref.1) | copy-start | bytes 24580

commit v4 on v3

--- a/solution.py
+++ b/solution.py
@@ -22,7 +22,9 @@
 ROW = 2 * NCH + 1
 SPLITS = 3
 FINE_SPLITS = 2
-ORDER = (37, 11, 21)
+LAGS1 = 4
+LAGS2 = 4
+ORDER = (57, 59, 57)
 
 
 def peer(i):
@@ -70,11 +72,14 @@
     return delay.astype(jnp.float32).astype(jnp.bfloat16)
 
 
-def one_hot(wide, width, groups):
-    lag = (lax.broadcasted_iota(jnp.int32, wide.shape, 1) // width) % 2
+def one_hot(wide, width, lags, groups):
+    lag = (lax.broadcasted_iota(jnp.int32, wide.shape, 1) // width) % lags
     wide = wide - lag.astype(jnp.float32)
     return jnp.concatenate(
-        [(wide == 2.0 * g).astype(jnp.float32).astype(jnp.bfloat16) for g in range(groups)],
+        [
+            (wide == float(lags * g)).astype(jnp.float32).astype(jnp.bfloat16)
+            for g in range(groups)
+        ],
         axis=0,
     )
 
@@ -104,10 +109,10 @@
     for d in range(D1):
         count = jnp.sum((delay == float(d)).astype(jnp.float32), axis=1, keepdims=True)
         counts = jnp.where(
-            jnp.logical_and(lane % D1 == d, lane < SPLITS * D1), count, counts
+            jnp.logical_and(lane % D1 == D1 - 1 - d, lane < SPLITS * D1), count, counts
         )
     out_ref[pl.ds(2 * NCH, NCOARSE, stride=ROW), :] = counts
-    weights = one_hot(jnp.concatenate([delay] * (2 * SPLITS), axis=1), SUBCH, D1 // 2)
+    weights = one_hot(jnp.concatenate([delay] * (LAGS1 * SPLITS), axis=1), SUBCH, LAGS1, D1 // LAGS1)
 
     copies[1].wait()
     keep = (1.0 - flags_ref[...].astype(jnp.float32)).astype(jnp.bfloat16)
@@ -135,12 +140,12 @@
             channel_sum, (NCOARSE, LANES)
         )
 
-    data = lag_rows(normed, 2, SPLITS, lane)
+    data = lag_rows(normed, LAGS1, SPLITS, lane)
     sums = jnp.dot(weights, data, preferred_element_type=jnp.float32)
     totals = None
-    for d in range(D1 // 2):
+    for d in range(D1 // LAGS1):
         part = sums[d * NCOARSE : (d + 1) * NCOARSE]
-        part = shifted([part[:, c * LANES : (c + 1) * LANES] for c in range(NCH)], 2 * d, lane)
+        part = shifted([part[:, c * LANES : (c + 1) * LANES] for c in range(NCH)], LAGS1 * d, lane)
         totals = part if totals is None else [a + b for a, b in zip(totals, part)]
     for c in range(NCH):
         out_ref[pl.ds(c, NCOARSE, stride=ROW), :] = totals[c]
@@ -160,12 +165,14 @@
     ]
     counts = moved_ref[pl.ds(2 * NCH, NSUB, stride=ROW), :]
 
-    lane8 = lane_ids(D1)
-    row8 = lax.broadcasted_iota(jnp.int32, (D1, LANES), 0)
-    later = zero
-    for d in range(1, D1):
-        moved_on = shifted(zero, d, lane8)
-        later = [jnp.where(row8 == d, moved_on[c], later[c]) for c in range(NCH)]
+    row = lax.broadcasted_iota(jnp.int32, (D1, LANES), 0)
+    rolled = [
+        pltpu.roll(z, LANES - (D1 - 1), axis=1, stride=1, stride_axis=0) for z in zero
+    ] + [jnp.zeros((D1, LANES), jnp.float32)]
+    later = [
+        jnp.where(lane_ids(D1) < LANES - (D1 - 1) + row, rolled[c], rolled[c + 1])
+        for c in range(NCH)
+    ]
     later = jnp.concatenate(later, axis=1)
     parts = [p.astype(jnp.float32) for p in pieces(later, SPLITS)]
     parts.append(jnp.zeros_like(parts[0]))
@@ -177,18 +184,18 @@
 
     wide = jnp.dot(
         small(delay_ref[...]),
-        selector((NSUB, 2 * FINE_SPLITS * NSUB), 1),
+        selector((NSUB, LAGS2 * FINE_SPLITS * NSUB), 1),
         preferred_element_type=jnp.float32,
     )
-    weights = one_hot(wide, NSUB, D2 // 2)
-    data = lag_rows(subbands, 2, FINE_SPLITS, lane)
+    weights = one_hot(wide, NSUB, LAGS2, D2 // LAGS2)
+    data = lag_rows(subbands, LAGS2, FINE_SPLITS, lane)
     sums = jnp.dot(weights, data, preferred_element_type=jnp.float32)
     lane32 = lane_ids(JDEV)
     series = None
-    for f in range(D2 // 2):
+    for f in range(D2 // LAGS2):
         part = sums[f * JDEV : (f + 1) * JDEV]
         part = shifted(
-            [part[:, c * LANES : (c + 1) * LANES] for c in range(NCH)], 2 * f, lane32
+            [part[:, c * LANES : (c + 1) * LANES] for c in range(NCH)], LAGS2 * f, lane32
         )
         series = part if series is None else [a + b for a, b in zip(series, part)]
 
@@ -245,6 +252,7 @@
     out_ref[...] = peak_ref[...] / sigma[:, :JDEV]
 
 
+NOISE_ORDER = [39, 20, 55, 48, 17, 0, 16, 50, 1, 33, 35, 9, 31, 49, 54, 36, 15, 11, 59, 3, 29, 19, 10, 30, 27, 34, 24, 44, 63, 7, 28, 12, 46, 47, 61, 45, 32, 21, 62, 25, 22, 60, 4, 56, 40, 52, 38, 37, 23, 18, 41, 6, 2, 51, 43, 8, 57, 26, 13, 58, 5, 14, 42, 53]
 GROUP = [[peer(i) for i in range(NCOARSE)]]
 VMEM = pl.BlockSpec(memory_space=pltpu.VMEM)
 SMEM = pl.BlockSpec(memory_space=pltpu.SMEM)
@@ -295,7 +303,7 @@
         compiler_params=PARAMS,
     )(pltpu.with_memory_space_constraint(widths, pltpu.SMEM), in_vmem(moved.reshape(lanes * ROW, LANES)), fine_delay)
     squares = lax.all_to_all(
-        square.reshape(lanes, 1, LANES), "lane", split_axis=0, concat_axis=0, tiled=True, axis_index_groups=GROUP
+        square.reshape(lanes, 1, LANES), "lane", split_axis=0, concat_axis=0, tiled=True, axis_index_groups=[NOISE_ORDER]
     )
     out = pl.pallas_call(
         last_kernel,

time: 49.8 us -> 47.1 us (0.946)
  blocking collectives: 45 us -> 42.5 us
    all_to_all x1, blocking collectives: 30.6 us -> 29.3 us  [body(): lax.all_to_all(message.reshape(lanes, 1, ROW * LANES), 'lane', split_axis...]
    all_to_all x1, blocking collectives: 14.4 us -> 13.2 us  [body(): lax.all_to_all(square.reshape(lanes, 1, LANES), 'lane', split_axis=0, con...]
where the time goes in v4:
time: 47.1 us; the launch traced here: 46.9 us
  blocking collectives  42.5 us (90%)
  Pallas kernels  4.44 us (9%)
    all_to_all x1, blocking collectives, body(): lax.all_to_all(message.reshape(lanes, 1, ROW * LANES), 'lane', split_axis...  29.3 us
    all_to_all x1, blocking collectives, body(): lax.all_to_all(square.reshape(lanes, 1, LANES), 'lane', split_axis=0, con...  13.2 us
    pallas_call x1, Pallas kernels, body(): pl.pallas_call(front_kernel, name='front', in_specs=[ANY, ANY, ANY, ANY],...  2.2 us
    pallas_call x1, Pallas kernels, body(): pl.pallas_call(fine_kernel, name='fine', in_specs=[SMEM, VMEM, VMEM], out...  1.62 us

profile of v4, /device:TPU:1, one launch (start us, length us, event | category | flops | bytes accessed | tf_op | source)
XLA Modules:
  0.0 46.9 jit_solution(17128478610480649895)
XLA Ops:
  0.0 2.2 %front.1 = (f32[1088,128]{1,0:T(8,128)S(1)}, s32[8]{0:T(128)S(4)}) custom-call(f32[4,64,1024]{2,1,0:T(8,128)} %power_hbm.1, s32[4,8,64]{2,1,0:T(8,128)} %bitcast.14, s32[64,64]{1,0:T(8,128)} %delay_hbm.1, s32[8]{0:T(128)} %widths_hbm.1), custom_call_target="tpu_custom_call" | custom-call | tf_op jit(solution)/shard_map/front/pallas_call | solution.py:273
  2.2 0.0 copy-start
  2.2 29.3 %all_to_all.10 = f32[64,1,2176]{2,1,0:T(1,128)S(1)} all-to-all(f32[64,1,2176]{2,1,0:T(1,128)S(1)} %bitcast.11), channel_id=1, replica_groups={{27,42,34,22,51,3,53,63,33,43,29,23,9,5,8,20,52,45,32,60,28,4,50,21,11,..., dimensions={0} | all-to-all | bytes 1114112 | tf_op jit(solution)/shard_map/all_to_all | solution.py:290
  31.5 0.0 copy-done
  31.5 1.6 %fine.1 = (f32[64,128]{1,0:T(8,128)S(1)}, f32[8,32]{1,0:T(8,128)S(1)}) custom-call(s32[8]{0:T(128)S(4)} %get-tuple-element.9.widths_ref, f32[1088,128]{1,0:T(8,128)S(1)} %bitcast.10, s32[32,64]{1,0:T(8,128)S(1)} %copy-done), custom_call_target="tpu_custom_call" | custom-call | tf_op jit(solution)/shard_map/fine/pallas_call | solution.py:293
  33.1 13.2 %all_to_all.11 = f32[64,1,128]{2,1,0:T(1,128)S(1)} all-to-all(f32[64,1,128]{2,1,0:T(1,128)S(1)} %bitcast.13), channel_id=1, replica_groups={{39,20,55,48,17,0,16,50,1,33,35,9,31,49,54,36,15,11,59,3,29,19,10,30,27..., dimensions={0} | all-to-all | bytes 65536 | tf_op jit(solution)/shard_map/all_to_all | solution.py:305
  46.3 0.6 %last.1 = f32[8,32]{1,0:T(8,128)} custom-call(f32[64,128]{1,0:T(8,128)S(1)} %bitcast.12, f32[8,32]{1,0:T(8,128)S(1)} %get-tuple-element.12.peak_ref), custom_call_target="tpu_custom_call" | custom-call | tf_op jit(solution)/shard_map/last/pallas_call | solution.py:308
Async XLA Ops:
  2.2 29.3 %copy-start = (s32[32,64]{1,0:T(8,128)S(1)}, s32[32,64]{1,0:T(8,128)}, u32[]{:S(2)}) copy-start(s32[32,64]{1,0:T(8,128)} %delay_ref.1) | copy-start | bytes 24580

commit v5 on v4

--- a/solution.py
+++ b/solution.py
@@ -24,7 +24,7 @@
 FINE_SPLITS = 2
 LAGS1 = 4
 LAGS2 = 4
-ORDER = (57, 59, 57)
+ORDER = (51, 17, 49)
 
 
 def peer(i):
@@ -252,7 +252,12 @@
     out_ref[...] = peak_ref[...] / sigma[:, :JDEV]
 
 
-NOISE_ORDER = [39, 20, 55, 48, 17, 0, 16, 50, 1, 33, 35, 9, 31, 49, 54, 36, 15, 11, 59, 3, 29, 19, 10, 30, 27, 34, 24, 44, 63, 7, 28, 12, 46, 47, 61, 45, 32, 21, 62, 25, 22, 60, 4, 56, 40, 52, 38, 37, 23, 18, 41, 6, 2, 51, 43, 8, 57, 26, 13, 58, 5, 14, 42, 53]
+NOISE_ORDER = [
+    57, 32, 24, 20, 31, 61, 17, 1, 53, 5, 10, 43, 44, 59, 0, 36,
+    4, 35, 38, 33, 14, 50, 51, 60, 18, 7, 11, 55, 22, 63, 39, 19,
+    30, 3, 54, 2, 27, 29, 58, 13, 45, 37, 34, 56, 16, 41, 25, 52,
+    49, 47, 62, 46, 23, 6, 15, 9, 28, 26, 40, 8, 42, 12, 48, 21,
+]
 GROUP = [[peer(i) for i in range(NCOARSE)]]
 VMEM = pl.BlockSpec(memory_space=pltpu.VMEM)
 SMEM = pl.BlockSpec(memory_space=pltpu.SMEM)

time: 47.1 us -> 46 us (0.977)
  blocking collectives: 42.5 us -> 41.4 us
    all_to_all x1, blocking collectives: 29.3 us -> 27.4 us  [body(): lax.all_to_all(message.reshape(lanes, 1, ROW * LANES), 'lane', split_axis...]
    all_to_all x1, blocking collectives: 13.2 us -> 14 us  [body(): lax.all_to_all(square.reshape(lanes, 1, LANES), 'lane', split_axis=0, con...]
where the time goes in v5:
time: 46 us; the launch traced here: 45.8 us
  blocking collectives  41.4 us (90%)
  Pallas kernels  4.44 us (10%)
    all_to_all x1, blocking collectives, body(): lax.all_to_all(message.reshape(lanes, 1, ROW * LANES), 'lane', split_axis...  27.4 us
    all_to_all x1, blocking collectives, body(): lax.all_to_all(square.reshape(lanes, 1, LANES), 'lane', split_axis=0, con...  14 us
    pallas_call x1, Pallas kernels, body(): pl.pallas_call(front_kernel, name='front', in_specs=[ANY, ANY, ANY, ANY],...  2.2 us
    pallas_call x1, Pallas kernels, body(): pl.pallas_call(fine_kernel, name='fine', in_specs=[SMEM, VMEM, VMEM], out...  1.62 us

profile of v5, /device:TPU:1, one launch (start us, length us, event | category | flops | bytes accessed | tf_op | source)
XLA Modules:
  0.0 45.8 jit_solution(6473121346898825412)
XLA Ops:
  0.0 2.2 %front.1 = (f32[1088,128]{1,0:T(8,128)S(1)}, s32[8]{0:T(128)S(4)}) custom-call(f32[4,64,1024]{2,1,0:T(8,128)} %power_hbm.1, s32[4,8,64]{2,1,0:T(8,128)} %bitcast.14, s32[64,64]{1,0:T(8,128)} %delay_hbm.1, s32[8]{0:T(128)} %widths_hbm.1), custom_call_target="tpu_custom_call" | custom-call | tf_op jit(solution)/shard_map/front/pallas_call | solution.py:278
  2.2 0.0 copy-start
  2.2 27.4 %all_to_all.10 = f32[64,1,2176]{2,1,0:T(1,128)S(1)} all-to-all(f32[64,1,2176]{2,1,0:T(1,128)S(1)} %bitcast.11), channel_id=1, replica_groups={{43,5,41,48,49,62,23,60,39,36,37,42,3,26,30,24,61,22,63,11,15,0,44,2,52..., dimensions={0} | all-to-all | bytes 1114112 | tf_op jit(solution)/shard_map/all_to_all | solution.py:295
  29.6 0.0 copy-done
  29.6 1.6 %fine.1 = (f32[64,128]{1,0:T(8,128)S(1)}, f32[8,32]{1,0:T(8,128)S(1)}) custom-call(s32[8]{0:T(128)S(4)} %get-tuple-element.9.widths_ref, f32[1088,128]{1,0:T(8,128)S(1)} %bitcast.10, s32[32,64]{1,0:T(8,128)S(1)} %copy-done), custom_call_target="tpu_custom_call" | custom-call | tf_op jit(solution)/shard_map/fine/pallas_call | solution.py:298
  31.2 14.0 %all_to_all.11 = f32[64,1,128]{2,1,0:T(1,128)S(1)} all-to-all(f32[64,1,128]{2,1,0:T(1,128)S(1)} %bitcast.13), channel_id=1, replica_groups={{57,32,24,20,31,61,17,1,53,5,10,43,44,59,0,36,4,35,38,33,14,50,51,60,18..., dimensions={0} | all-to-all | bytes 65536 | tf_op jit(solution)/shard_map/all_to_all | solution.py:310
  45.2 0.6 %last.1 = f32[8,32]{1,0:T(8,128)} custom-call(f32[64,128]{1,0:T(8,128)S(1)} %bitcast.12, f32[8,32]{1,0:T(8,128)S(1)} %get-tuple-element.12.peak_ref), custom_call_target="tpu_custom_call" | custom-call | tf_op jit(solution)/shard_map/last/pallas_call | solution.py:313
Async XLA Ops:
  2.2 27.4 %copy-start = (s32[32,64]{1,0:T(8,128)S(1)}, s32[32,64]{1,0:T(8,128)}, u32[]{:S(2)}) copy-start(s32[32,64]{1,0:T(8,128)} %delay_ref.1) | copy-start | bytes 24580

commit v6 on v5

--- a/solution.py
+++ b/solution.py
@@ -24,7 +24,7 @@
 FINE_SPLITS = 2
 LAGS1 = 4
 LAGS2 = 4
-ORDER = (51, 17, 49)
+ORDER = (49, 44, 43)
 
 
 def peer(i):

time: 46 us -> 45.6 us (level)
  no operation moved by 1% of the time
where the time goes in v6:
time: 45.6 us; the launch traced here: 45.4 us
  blocking collectives  41 us (90%)
  Pallas kernels  4.45 us (10%)
    all_to_all x1, blocking collectives, body(): lax.all_to_all(message.reshape(lanes, 1, ROW * LANES), 'lane', split_axis...  27.4 us
    all_to_all x1, blocking collectives, body(): lax.all_to_all(square.reshape(lanes, 1, LANES), 'lane', split_axis=0, con...  13.6 us
    pallas_call x1, Pallas kernels, body(): pl.pallas_call(front_kernel, name='front', in_specs=[ANY, ANY, ANY, ANY],...  2.2 us
    pallas_call x1, Pallas kernels, body(): pl.pallas_call(fine_kernel, name='fine', in_specs=[SMEM, VMEM, VMEM], out...  1.62 us

profile of v6, /device:TPU:1, one launch (start us, length us, event | category | flops | bytes accessed | tf_op | source)
XLA Modules:
  0.0 45.4 jit_solution(6133313823575832658)
XLA Ops:
  0.0 2.2 %front.1 = (f32[1088,128]{1,0:T(8,128)S(1)}, s32[8]{0:T(128)S(4)}) custom-call(f32[4,64,1024]{2,1,0:T(8,128)} %power_hbm.1, s32[4,8,64]{2,1,0:T(8,128)} %bitcast.14, s32[64,64]{1,0:T(8,128)} %delay_hbm.1, s32[8]{0:T(128)} %widths_hbm.1), custom_call_target="tpu_custom_call" | custom-call | tf_op jit(solution)/shard_map/front/pallas_call | solution.py:278
  2.2 0.0 copy-start
  2.2 27.4 %all_to_all.10 = f32[64,1,2176]{2,1,0:T(1,128)S(1)} all-to-all(f32[64,1,2176]{2,1,0:T(1,128)S(1)} %bitcast.11), channel_id=1, replica_groups={{43,8,4,34,22,58,60,1,47,9,27,38,16,45,63,37,35,54,24,28,0,50,42,29,39,..., dimensions={0} | all-to-all | bytes 1114112 | tf_op jit(solution)/shard_map/all_to_all | solution.py:295
  29.6 0.0 copy-done
  29.6 1.6 %fine.1 = (f32[64,128]{1,0:T(8,128)S(1)}, f32[8,32]{1,0:T(8,128)S(1)}) custom-call(s32[8]{0:T(128)S(4)} %get-tuple-element.9.widths_ref, f32[1088,128]{1,0:T(8,128)S(1)} %bitcast.10, s32[32,64]{1,0:T(8,128)S(1)} %copy-done), custom_call_target="tpu_custom_call" | custom-call | tf_op jit(solution)/shard_map/fine/pallas_call | solution.py:298
  31.2 13.6 %all_to_all.11 = f32[64,1,128]{2,1,0:T(1,128)S(1)} all-to-all(f32[64,1,128]{2,1,0:T(1,128)S(1)} %bitcast.13), channel_id=1, replica_groups={{57,32,24,20,31,61,17,1,53,5,10,43,44,59,0,36,4,35,38,33,14,50,51,60,18..., dimensions={0} | all-to-all | bytes 65536 | tf_op jit(solution)/shard_map/all_to_all | solution.py:310
  44.8 0.6 %last.1 = f32[8,32]{1,0:T(8,128)} custom-call(f32[64,128]{1,0:T(8,128)S(1)} %bitcast.12, f32[8,32]{1,0:T(8,128)S(1)} %get-tuple-element.12.peak_ref), custom_call_target="tpu_custom_call" | custom-call | tf_op jit(solution)/shard_map/last/pallas_call | solution.py:313
Async XLA Ops:
  2.2 27.4 %copy-start = (s32[32,64]{1,0:T(8,128)S(1)}, s32[32,64]{1,0:T(8,128)}, u32[]{:S(2)}) copy-start(s32[32,64]{1,0:T(8,128)} %delay_ref.1) | copy-start | bytes 24580
